TPU v7x, 32 devices: a 4x4x1 block of a 4x4x8 slice. The times are simulated.
32 devices in a mesh: dp: 1 (over z), cp: 4 (over y), tp: 8 (over x, core).
Axes of the slice: x: 4, y: 4, z: 1, core: 2. Of those that a mesh axis runs over, the one named last changes fastest.
The devices are a block of a 4x4x8 slice.
Arguments:
- x: bfloat16 [1, 8192, 5120], P('dp', ('cp', 'tp'))
- g_attn: bfloat16 [5120], replicated
- w_q: bfloat16 [5120, 40, 128], P(None, 'tp')
- w_k: bfloat16 [5120, 8, 128], P(None, 'tp')
- w_v: bfloat16 [5120, 8, 128], P(None, 'tp')
- w_o: bfloat16 [40, 128, 5120], P('tp')
- g_mlp: bfloat16 [5120], replicated
- w_gate: bfloat16 [5120, 27648], P(None, 'tp')
- w_up: bfloat16 [5120, 27648], P(None, 'tp')
- w_down: bfloat16 [27648, 5120], P('tp')
Outputs:
- output: bfloat16 [1, 8192, 5120], P('dp', ('cp', 'tp'))
All inputs are finite; a program needn't handle non-finite values.
Results may differ from a plain program's by a relative error of at most 0.02.
Values are sent between devices in bfloat16 or wider.
A program may use at most 768 MiB of HBM per device.

v0:
```python
import jax
import jax.numpy as jnp
from jax import lax
from jax.sharding import PartitionSpec as P

NORM_EPS = 1e-5
ROPE_THETA = 500000.0
TILE_ROWS = 256


def rms_norm(rows_in, gain_vec):
    rows_f32 = rows_in.astype(jnp.float32)
    mean_sq = jnp.mean(rows_f32 * rows_f32, axis=-1, keepdims=True)
    return (rows_f32 * lax.rsqrt(mean_sq + NORM_EPS) * gain_vec.astype(jnp.float32)).astype(jnp.bfloat16)


def apply_rope(heads_in, positions):
    head_dim = heads_in.shape[-1]
    half_dim = head_dim // 2
    inv_freq = ROPE_THETA ** (-2.0 * jnp.arange(half_dim, dtype=jnp.float32) / head_dim)
    angles = positions.astype(jnp.float32)[:, None] * inv_freq[None, :]
    angles = jnp.concatenate([angles, angles], axis=-1)[:, None, :]
    heads_f32 = heads_in.astype(jnp.float32)
    rotated = jnp.concatenate([-heads_f32[..., half_dim:], heads_f32[..., :half_dim]], axis=-1)
    return (heads_f32 * jnp.cos(angles) + rotated * jnp.sin(angles)).astype(jnp.bfloat16)


def stored_positions(row_ids, piece_len, cp_size):
    owner_cp = row_ids // (2 * piece_len)
    within = row_ids % (2 * piece_len)
    return jnp.where(within < piece_len, owner_cp * piece_len + within,
                     (2 * cp_size - 1 - owner_cp) * piece_len + within - piece_len)


def attend(q_rows, q_pos, keys, values, key_pos):
    q_len, n_kv_heads, group_size, head_dim = q_rows.shape
    n_tiles = max(1, q_len // TILE_ROWS)
    tile_len = q_len // n_tiles
    score_scale = head_dim ** -0.5

    def one_tile(tile_idx):
        row_start = tile_idx * tile_len
        q_tile = lax.dynamic_slice_in_dim(q_rows, row_start, tile_len, axis=0)
        pos_tile = lax.dynamic_slice_in_dim(q_pos, row_start, tile_len, axis=0)
        scores = jnp.einsum('qgrd,kgd->gqrk', q_tile, keys, preferred_element_type=jnp.float32) * score_scale
        visible = pos_tile[:, None, None] >= key_pos[None, None, :]
        scores = jnp.where(visible, scores, -1e30)
        weights = jnp.exp(scores - jnp.max(scores, axis=-1, keepdims=True))
        row_sum = jnp.sum(weights, axis=-1, keepdims=True)
        mixed_vals = jnp.einsum('gqrk,kgd->gqrd', weights.astype(jnp.bfloat16), values, preferred_element_type=jnp.float32) / row_sum
        return jnp.transpose(mixed_vals, (1, 0, 2, 3)).astype(jnp.bfloat16)

    tiles = lax.map(one_tile, jnp.arange(n_tiles))
    return tiles.reshape(q_len, n_kv_heads * group_size, head_dim)


def solution(mesh):
    cp_size = mesh.shape['cp']
    row_spec = P('dp', ('cp', 'tp'), None)
    head_cols = P(None, 'tp', None)

    def local_layer(x, g_attn, w_q, w_k, w_v, w_o, g_mlp, w_gate, w_up, w_down):
        x_rows = x[0]
        n_kv_local = w_k.shape[1]
        head_dim = w_q.shape[2]
        group_size = w_q.shape[1] // n_kv_local
        cp_index = lax.axis_index('cp')
        normed = lax.all_gather(rms_norm(x_rows, g_attn), 'tp', axis=0, tiled=True)
        seq_local = normed.shape[0]
        piece_len = seq_local // 2
        positions = stored_positions(cp_index * seq_local + jnp.arange(seq_local, dtype=jnp.int32), piece_len, cp_size)
        q_all = apply_rope(jnp.einsum('sd,dhk->shk', normed, w_q, preferred_element_type=jnp.float32).astype(jnp.bfloat16), positions)
        k_all = apply_rope(jnp.einsum('sd,dhk->shk', normed, w_k, preferred_element_type=jnp.float32).astype(jnp.bfloat16), positions)
        v_all = jnp.einsum('sd,dhk->shk', normed, w_v, preferred_element_type=jnp.float32).astype(jnp.bfloat16)
        k_seq = lax.all_gather(k_all, 'cp', axis=0, tiled=False)
        v_seq = lax.all_gather(v_all, 'cp', axis=0, tiled=False)
        key_pos = stored_positions(jnp.arange(cp_size * seq_local, dtype=jnp.int32), piece_len, cp_size).reshape(cp_size, seq_local)
        first_keys = k_seq[:, :piece_len].reshape(cp_size * piece_len, n_kv_local, head_dim)
        first_vals = v_seq[:, :piece_len].reshape(cp_size * piece_len, n_kv_local, head_dim)
        first_pos = key_pos[:, :piece_len].reshape(cp_size * piece_len)
        q_grp = q_all.reshape(seq_local, n_kv_local, group_size, head_dim)
        attn_first = attend(q_grp[:piece_len], positions[:piece_len], first_keys, first_vals, first_pos)
        attn_second = attend(q_grp[piece_len:], positions[piece_len:],
                             k_seq.reshape(cp_size * seq_local, n_kv_local, head_dim),
                             v_seq.reshape(cp_size * seq_local, n_kv_local, head_dim),
                             key_pos.reshape(cp_size * seq_local))
        attn_out = jnp.concatenate([attn_first, attn_second], axis=0)
        attn_part = jnp.einsum('shk,hkd->sd', attn_out, w_o, preferred_element_type=jnp.float32).astype(jnp.bfloat16)
        attn_rows = lax.psum_scatter(attn_part, 'tp', scatter_dimension=0, tiled=True)
        resid_rows = (x_rows.astype(jnp.float32) + attn_rows.astype(jnp.float32)).astype(jnp.bfloat16)
        normed_mlp = lax.all_gather(rms_norm(resid_rows, g_mlp), 'tp', axis=0, tiled=True)
        gate_proj = jnp.dot(normed_mlp, w_gate, preferred_element_type=jnp.float32)
        up_proj = jnp.dot(normed_mlp, w_up, preferred_element_type=jnp.float32)
        hidden = (jax.nn.silu(gate_proj) * up_proj).astype(jnp.bfloat16)
        down_part = jnp.dot(hidden, w_down, preferred_element_type=jnp.float32).astype(jnp.bfloat16)
        down_rows = lax.psum_scatter(down_part, 'tp', scatter_dimension=0, tiled=True)
        z_rows = (resid_rows.astype(jnp.float32) + down_rows.astype(jnp.float32)).astype(jnp.bfloat16)
        return z_rows[None]

    return jax.shard_map(local_layer, mesh=mesh,
                         in_specs=(row_spec, P(), head_cols, head_cols, head_cols, P('tp', None, None),
                                   P(), P(None, 'tp'), P(None, 'tp'), P('tp', None)),
                         out_specs=row_spec, check_vma=False)
```

profile of v0, /device:TPU:97, one launch (start us, length us, event | category | flops | bytes accessed | tf_op | source)
XLA Modules:
  0.0 1152.6 jit_solution(15179440924207427082)
XLA Ops:
  6.6 2.4 fusion.89
  9.7 4.0 fusion.91
  14.6 104.1 %all-gather.7.cloned.1.call-done = bf16[2048,5120]{1,0:T(8,128)(2,1)} async-done(((bf16[256,5120]{1,0:T(8,128)(2,1)}), bf16[2048,5120]{1,0:T(8,128)(2,1)}) %all-gather.7.cloned.1.call-update) | async-done | bytes 20971536 | tf_op jit(solution)/shard_map/all_gather | solution.py:68
  118.7 10.7 convolution_convert_fusion.1
  129.5 9.6 copy.11
  139.3 11.2 fusion.99
  150.6 5.2 fusion.105
  156.1 18.8 %fusion.117 = f32[2048,640]{0,1:S(1)} fusion(bf16[2048,5120]{1,0:T(8,128)(2,1)} %all-gather.7.cloned.1.call-done, bf16[5120,640]{0,1:T(8,128)(2,1)} %bitcast.147), kind=kOutput, calls=%fused_computation.136 | convolution fusion | flops 13421772800 | bytes 32768000
  176.8 3.1 fusion.94
  179.8 3.4 slice_bitcast_fusion.1
  187.3 4.2 copy.16
  191.5 2.8 reshape.296
  198.3 81.9 %while.21 = (s32[]{:T(128)}, bf16[4,256,1,5,128]{4,1,0,3,2:T(8,128)(2,1)}, s32[4]{0:T(128)S(1)}, s32[1024]{0:T(1024)S(1)}, s32[4,1024]{1,0:T(4,128)S(1)}, /*inde...) while((s32[]{:T(128)}, ...), condition=%wide.region_4.5_spmd, body=%wide.region_1.4_spmd.sunk | while | flops 2743399936 | bytes 69939400 | solution.py:53
  200.5 5.3 fusion.143
  205.8 5.9 fusion.144
  211.7 7.2 fusion.145
  220.9 5.3 fusion.143
  226.2 5.9 fusion.144
  232.1 7.3 fusion.145
  241.3 5.3 fusion.143
  246.6 5.9 fusion.144
  252.5 7.2 fusion.145
  261.7 5.3 fusion.143
  267.0 5.9 fusion.144
  272.9 7.3 fusion.145
  281.5 242.1 %while.22 = (s32[]{:T(128)}, bf16[4,256,1,5,128]{4,1,0,3,2:T(8,128)(2,1)}, s32[4]{0:T(128)S(1)}, s32[1024]{0:T(1024)}, bf16[1024,1,5,128]{0,3,2,1:T(8,128)(2,1)}...) while((s32[]{:T(128)}, ...), condition=%wide.region_8.9_spmd.clone, body=%wide.region_5.8_spmd.clone.sunk | while | flops 5486638592 | bytes 139161808 | solution.py:53
  285.2 19.2 %fusion.149 = (f32[256,5]{0,1:T(8,128)S(1)}, f32[256,5,8192]{2,0,1:T(8,128)}) fusion(pred[256,8192]{1,0:T(8,128)(4,1)S(1)} %broadcast_compare_fusion.6, bf16[8192,1,128]{2,0,1:T(8,128)(2,1)} %get-tuple-element.298, bf16[1024,1,5,128]{0,3,2,1:T(8,128)(2,1)} %get-tuple-element.297, s32[]{:T(128)S(6)} %select_n.207), kind=kOutput, calls=%fused_computation.24.clone.1 | convolution fusion | flops 2715810560 | bytes 46470148 | tf_op jit(solution)/shard_map/while/body/eval_jaxpr/qgrd,kgd->gqrk/dot_general | solution.py:45
  304.4 18.9 %fusion.150 = f32[256,5]{0,1:T(8,128)S(1)} fusion(f32[256,5,8192]{2,0,1:T(8,128)} %get-tuple-element.269, f32[256,5]{0,1:T(8,128)S(1)} %get-tuple-element.270, pred[256,8192]{1,0:T(8,128)(4,1)S(1)} %broadcast_compare_fusion.6), kind=kLoop, calls=%fused_computation.25.clone.1 | loop fusion | flops 41941760 | bytes 44050432 | tf_op jit(solution)/shard_map/while/body/eval_jaxpr/reduce_sum | solution.py:49
  323.2 19.2 %fusion.151 = bf16[4,256,1,5,128]{4,1,0,3,2:T(8,128)(2,1)} fusion(bf16[4,256,1,5,128]{4,1,0,3,2:T(8,128)(2,1)} %get-tuple-element.283, s32[]{:T(128)S(6)} %copy.33, bf16[8192,1,128]{2,0,1:T(8,128)(2,1)} %get-tuple-element.299, f32[256,5,8192]{2,0,1:T(8,128)} %get-tuple-element.269, f32[256,5]{0,1:T(8,128)S(1)} %get-tuple-element.270, ...), kind=kOutput, calls=%fused_computation.36.clone.1 | convolution fusion | flops 2726625280 | bytes 46475268 | tf_op jit(solution)/shard_map/while/body/eval_jaxpr/gqrk,kgd->gqrd/dot_general | solution.py:50
  345.6 19.2 %fusion.149 = (f32[256,5]{0,1:T(8,128)S(1)}, f32[256,5,8192]{2,0,1:T(8,128)}) fusion(pred[256,8192]{1,0:T(8,128)(4,1)S(1)} %broadcast_compare_fusion.6, bf16[8192,1,128]{2,0,1:T(8,128)(2,1)} %get-tuple-element.298, bf16[1024,1,5,128]{0,3,2,1:T(8,128)(2,1)} %get-tuple-element.297, s32[]{:T(128)S(6)} %select_n.207), kind=kOutput, calls=%fused_computation.24.clone.1 | convolution fusion | flops 2715810560 | bytes 46470148 | tf_op jit(solution)/shard_map/while/body/eval_jaxpr/qgrd,kgd->gqrk/dot_general | solution.py:45
  364.8 18.9 %fusion.150 = f32[256,5]{0,1:T(8,128)S(1)} fusion(f32[256,5,8192]{2,0,1:T(8,128)} %get-tuple-element.269, f32[256,5]{0,1:T(8,128)S(1)} %get-tuple-element.270, pred[256,8192]{1,0:T(8,128)(4,1)S(1)} %broadcast_compare_fusion.6), kind=kLoop, calls=%fused_computation.25.clone.1 | loop fusion | flops 41941760 | bytes 44050432 | tf_op jit(solution)/shard_map/while/body/eval_jaxpr/reduce_sum | solution.py:49
  383.7 19.1 %fusion.151 = bf16[4,256,1,5,128]{4,1,0,3,2:T(8,128)(2,1)} fusion(bf16[4,256,1,5,128]{4,1,0,3,2:T(8,128)(2,1)} %get-tuple-element.283, s32[]{:T(128)S(6)} %copy.33, bf16[8192,1,128]{2,0,1:T(8,128)(2,1)} %get-tuple-element.299, f32[256,5,8192]{2,0,1:T(8,128)} %get-tuple-element.269, f32[256,5]{0,1:T(8,128)S(1)} %get-tuple-element.270, ...), kind=kOutput, calls=%fused_computation.36.clone.1 | convolution fusion | flops 2726625280 | bytes 46475268 | tf_op jit(solution)/shard_map/while/body/eval_jaxpr/gqrk,kgd->gqrd/dot_general | solution.py:50
  406.1 19.1 %fusion.149 = (f32[256,5]{0,1:T(8,128)S(1)}, f32[256,5,8192]{2,0,1:T(8,128)}) fusion(pred[256,8192]{1,0:T(8,128)(4,1)S(1)} %broadcast_compare_fusion.6, bf16[8192,1,128]{2,0,1:T(8,128)(2,1)} %get-tuple-element.298, bf16[1024,1,5,128]{0,3,2,1:T(8,128)(2,1)} %get-tuple-element.297, s32[]{:T(128)S(6)} %select_n.207), kind=kOutput, calls=%fused_computation.24.clone.1 | convolution fusion | flops 2715810560 | bytes 46470148 | tf_op jit(solution)/shard_map/while/body/eval_jaxpr/qgrd,kgd->gqrk/dot_general | solution.py:45
  425.2 18.9 %fusion.150 = f32[256,5]{0,1:T(8,128)S(1)} fusion(f32[256,5,8192]{2,0,1:T(8,128)} %get-tuple-element.269, f32[256,5]{0,1:T(8,128)S(1)} %get-tuple-element.270, pred[256,8192]{1,0:T(8,128)(4,1)S(1)} %broadcast_compare_fusion.6), kind=kLoop, calls=%fused_computation.25.clone.1 | loop fusion | flops 41941760 | bytes 44050432 | tf_op jit(solution)/shard_map/while/body/eval_jaxpr/reduce_sum | solution.py:49
  444.1 19.1 %fusion.151 = bf16[4,256,1,5,128]{4,1,0,3,2:T(8,128)(2,1)} fusion(bf16[4,256,1,5,128]{4,1,0,3,2:T(8,128)(2,1)} %get-tuple-element.283, s32[]{:T(128)S(6)} %copy.33, bf16[8192,1,128]{2,0,1:T(8,128)(2,1)} %get-tuple-element.299, f32[256,5,8192]{2,0,1:T(8,128)} %get-tuple-element.269, f32[256,5]{0,1:T(8,128)S(1)} %get-tuple-element.270, ...), kind=kOutput, calls=%fused_computation.36.clone.1 | convolution fusion | flops 2726625280 | bytes 46475268 | tf_op jit(solution)/shard_map/while/body/eval_jaxpr/gqrk,kgd->gqrd/dot_general | solution.py:50
  466.5 19.2 %fusion.149 = (f32[256,5]{0,1:T(8,128)S(1)}, f32[256,5,8192]{2,0,1:T(8,128)}) fusion(pred[256,8192]{1,0:T(8,128)(4,1)S(1)} %broadcast_compare_fusion.6, bf16[8192,1,128]{2,0,1:T(8,128)(2,1)} %get-tuple-element.298, bf16[1024,1,5,128]{0,3,2,1:T(8,128)(2,1)} %get-tuple-element.297, s32[]{:T(128)S(6)} %select_n.207), kind=kOutput, calls=%fused_computation.24.clone.1 | convolution fusion | flops 2715810560 | bytes 46470148 | tf_op jit(solution)/shard_map/while/body/eval_jaxpr/qgrd,kgd->gqrk/dot_general | solution.py:45
  485.6 18.9 %fusion.150 = f32[256,5]{0,1:T(8,128)S(1)} fusion(f32[256,5,8192]{2,0,1:T(8,128)} %get-tuple-element.269, f32[256,5]{0,1:T(8,128)S(1)} %get-tuple-element.270, pred[256,8192]{1,0:T(8,128)(4,1)S(1)} %broadcast_compare_fusion.6), kind=kLoop, calls=%fused_computation.25.clone.1 | loop fusion | flops 41941760 | bytes 44050432 | tf_op jit(solution)/shard_map/while/body/eval_jaxpr/reduce_sum | solution.py:49
  504.5 19.2 %fusion.151 = bf16[4,256,1,5,128]{4,1,0,3,2:T(8,128)(2,1)} fusion(bf16[4,256,1,5,128]{4,1,0,3,2:T(8,128)(2,1)} %get-tuple-element.283, s32[]{:T(128)S(6)} %copy.33, bf16[8192,1,128]{2,0,1:T(8,128)(2,1)} %get-tuple-element.299, f32[256,5,8192]{2,0,1:T(8,128)} %get-tuple-element.269, f32[256,5]{0,1:T(8,128)S(1)} %get-tuple-element.270, ...), kind=kOutput, calls=%fused_computation.36.clone.1 | convolution fusion | flops 2726625280 | bytes 46475268 | tf_op jit(solution)/shard_map/while/body/eval_jaxpr/gqrk,kgd->gqrd/dot_general | solution.py:50
  523.6 22.0 %bitcast_convert_fusion = bf16[2048,5120]{1,0:T(8,128)(2,1)} fusion(bf16[5,128,5120]{2,1,0:T(8,128)(2,1)} %param.19, bf16[1024,5,128]{2,0,1:T(8,128)(2,1)} %bitcast.149, bf16[1024,5,128]{2,0,1:T(8,128)(2,1)} %bitcast.150), kind=kOutput, calls=%fused_computation.61 | convolution fusion | flops 13437501440 | bytes 30146560 | tf_op jit(solution)/shard_map/shk,hkd->sd/dot_general | solution.py:88
  546.3 108.3 %reduce-scatter.3.cloned.1.call-done = bf16[256,5120]{1,0:T(8,128)(2,1)} async-done(((bf16[2048,5120]{1,0:T(8,128)(2,1)}), bf16[256,5120]{1,0:T(8,128)(2,1)}) %reduce-scatter.3.cloned.1.call-update) | async-done | bytes 2621456 | tf_op jit(solution)/shard_map/reduce_scatter | solution.py:89
  654.6 3.6 fusion.85
  658.2 4.4 fusion.87
  662.8 101.0 %all-gather.9.cloned.1.call-done = bf16[2048,5120]{1,0:T(8,128)(2,1)} async-done(((bf16[256,5120]{1,0:T(8,128)(2,1)}), bf16[2048,5120]{1,0:T(8,128)(2,1)}) %all-gather.9.cloned.1.call-update) | async-done | bytes 20971536 | tf_op jit(solution)/shard_map/all_gather | solution.py:91
  763.9 87.8 %fusion.118 = f32[2048,3456]{1,0:T(8,128)} fusion(bf16[2048,5120]{1,0:T(8,128)(2,1)} %all-gather.9.cloned.1.call-done, bf16[5120,3456]{1,0:T(8,128)(2,1)} %param.21), kind=kOutput, calls=%fused_computation.137 | convolution fusion | flops 72477573120 | bytes 84672512 | tf_op jit(solution)/shard_map/dot_general | solution.py:92
  851.6 93.7 %multiply_convert_fusion = bf16[2048,3456]{1,0:T(8,128)(2,1)} fusion(f32[2048,3456]{1,0:T(8,128)} %fusion.118, bf16[2048,5120]{1,0:T(8,128)(2,1)} %all-gather.9.cloned.1.call-done, bf16[5120,3456]{1,0:T(8,128)(2,1)} %param.22), kind=kOutput, calls=%fused_computation.62 | convolution fusion | flops 72520040448 | bytes 98828288 | tf_op jit(solution)/shard_map/dot_general | solution.py:93
  945.4 84.6 %convolution_convert_fusion = bf16[2048,5120]{1,0:T(8,128)(2,1)} fusion(bf16[2048,3456]{1,0:T(8,128)(2,1)} %multiply_convert_fusion, bf16[3456,5120]{1,0:T(8,128)(2,1)} %param.23), kind=kOutput, calls=%fused_computation.63 | convolution fusion | flops 72488058880 | bytes 70516736 | tf_op jit(solution)/shard_map/dot_general | solution.py:95
  1030.1 109.1 %reduce-scatter.5.cloned.1.call-done = bf16[256,5120]{1,0:T(8,128)(2,1)} async-done(((bf16[2048,5120]{1,0:T(8,128)(2,1)}), bf16[256,5120]{1,0:T(8,128)(2,1)}) %reduce-scatter.5.cloned.1.call-update) | async-done | bytes 2621456 | tf_op jit(solution)/shard_map/reduce_scatter | solution.py:96
  1139.2 6.1 fusion.95
  (83 shorter events, 30.0 us)
Async XLA Ops:
  6.5 112.1 %copy-start = (bf16[5120,1,128]{2,0,1:T(8,128)(2,1)S(1)}, bf16[5120,1,128]{2,0,1:T(8,128)(2,1)}, u32[]{:S(2)}) copy-start(bf16[5120,1,128]{2,0,1:T(8,128)(2,1)} %param.18) | copy-start | bytes 3932164
  6.6 112.1 %all-gather.7.cloned.1.call-start = ((), (), s32[]{:S(2)}) async-start(), calls=%async_computation.2 | async-start | bytes 23592960 | tf_op jit(solution)/shard_map/all_gather | solution.py:68
  13.8 169.5 %all-gather.13.cloned.1.call-start = ((), (), s32[]{:S(2)}) async-start(), calls=%async_computation.7 | async-start | bytes 2621440 | tf_op jit(solution)/shard_map/all_gather | solution.py:76
  129.4 57.9 %all-gather.11.cloned.1.call-start = ((), (), s32[]{:S(2)}) async-start(), calls=%async_computation.6 | async-start | bytes 2621440 | tf_op jit(solution)/shard_map/all_gather | solution.py:75
  129.5 9.8 copy-start.5
  155.9 498.7 %reduce-scatter.3.cloned.1.call-start = ((), (), s32[]{:S(2)}) async-start(), calls=%async_computation.3 | async-start | bytes 23592960 | tf_op jit(solution)/shard_map/reduce_scatter | solution.py:89
  175.5 1.2 copy-start.4
  187.3 4.2 copy-start.3
  545.6 0.7 copy-start.6
  545.7 218.2 %all-gather.9.cloned.1.call-start = ((), (), s32[]{:S(2)}) async-start(), calls=%async_computation.4 | async-start | bytes 23592960 | tf_op jit(solution)/shard_map/all_gather | solution.py:91
  654.6 3.6 copy-start.2
  662.7 476.4 %reduce-scatter.5.cloned.1.call-start = ((), (), s32[]{:S(2)}) async-start(), calls=%async_computation.5 | async-start | bytes 23592960 | tf_op jit(solution)/shard_map/reduce_scatter | solution.py:96
  1030.1 115.2 %copy-start.1 = (bf16[5120,1,128]{2,0,1:T(8,128)(2,1)S(1)}, bf16[5120,1,128]{2,0,1:T(8,128)(2,1)}, u32[]{:S(2)}) copy-start(bf16[5120,1,128]{2,0,1:T(8,128)(2,1)} %param.18) | copy-start | bytes 3932164
Sparse Core Ops, SparseCore 0:
  13.9 104.7 all-gather.6
  129.5 28.1 all-gather.12
  159.3 27.9 all-gather.10
  545.8 108.7 reduce-scatter.2
  662.9 100.9 all-gather.8
  1030.2 108.9 reduce-scatter.4
where the time goes:
time: 1160 us; the launch traced here: 1150 us
  matrix products  532 us (46%)
  waiting for transfers between devices  425 us (37%)
  other arithmetic  138 us (12%)
  local copies, waits for them, and re-layouts  37.5 us (3%)
  between operations  14.1 us (1%)
    reduce_scatter x1, waiting for transfers between devices, local_layer(): lax.psum_scatter(down_part, 'tp', scatter_dimension=0, tiled=True)  109 us
    reduce_scatter x1, waiting for transfers between devices, local_layer(): lax.psum_scatter(attn_part, 'tp', scatter_dimension=0, tiled=True)  108 us
    dot_general x8, matrix products, one_tile(): jnp.einsum('gqrk,kgd->gqrd', weights.astype(jnp.bfloat16), values, prefer...  106 us
    all_gather x1, waiting for transfers between devices, local_layer(): normed = lax.all_gather(rms_norm(x_rows, g_attn), 'tp', axis=0, tiled=True)  104 us
    all_gather x1, waiting for transfers between devices, local_layer(): lax.all_gather(rms_norm(resid_rows, g_mlp), 'tp', axis=0, tiled=True)  101 us
    reduce_sum x8, other arithmetic, one_tile(): row_sum = jnp.sum(weights, axis=-1, keepdims=True)  99.1 us
    dot_general x8, matrix products, one_tile(): jnp.einsum('qgrd,kgd->gqrk', q_tile, keys, preferred_element_type=jnp.flo...  97.8 us
    dot_general x1, matrix products, local_layer(): up_proj = jnp.dot(normed_mlp, w_up, preferred_element_type=jnp.float32)  93.7 us
  transfers between devices with their start and end apart: 6, of which 5 were waited for; matrix products, arithmetic and copies ran while one was open for 5% of the time, Pallas kernels for 0%

commit v1 on v0

v1 whole, which is shorter than its diff:
```python
import functools
import jax
import jax.numpy as jnp
from jax import lax
from jax.experimental import pallas as pl
from jax.experimental.pallas import tpu as pltpu
from jax.sharding import PartitionSpec as P

NORM_EPS = 1e-5
ROPE_THETA = 500000.0
LOG2_E = 1.4426950408889634
N_CHUNKS = 2
MLP_CHUNKS = 4


def rms_norm(rows_in, gain_vec):
    rows_f32 = rows_in.astype(jnp.float32)
    mean_sq = jnp.mean(rows_f32 * rows_f32, axis=-1, keepdims=True)
    return (rows_f32 * lax.rsqrt(mean_sq + NORM_EPS) * gain_vec.astype(jnp.float32)).astype(jnp.bfloat16)


def rope_tables(positions, head_dim):
    half_dim = head_dim // 2
    inv_freq = ROPE_THETA ** (-2.0 * jnp.arange(half_dim, dtype=jnp.float32) / head_dim)
    angles = positions.astype(jnp.float32)[:, None] * inv_freq[None, :]
    cos, sin = jnp.cos(angles), jnp.sin(angles)
    return jnp.concatenate([cos, cos], axis=-1), jnp.concatenate([-sin, sin], axis=-1)


def qkv_kernel(x_ref, wq_ref, wk_ref, wv_ref, cos_ref, sin_ref, q_ref, kv_ref):
    n_heads, head_dim = wq_ref.shape[0], wq_ref.shape[2]
    weights = jnp.concatenate([wk_ref[0], wv_ref[0]] + [wq_ref[h] for h in range(n_heads)], axis=1)
    out = jnp.dot(x_ref[...], weights, preferred_element_type=jnp.float32).astype(jnp.bfloat16)
    keys = out[:, :head_dim].astype(jnp.float32)
    keys = keys * cos_ref[...] + pltpu.roll(keys, head_dim // 2, 1) * sin_ref[...]
    kv_ref[:, :head_dim] = keys.astype(jnp.bfloat16)
    kv_ref[:, head_dim:] = out[:, head_dim:2 * head_dim]
    q_ref[...] = out[:, 2 * head_dim:]


def project_qkv(x, w_q, w_k, w_v, cos, sin):
    rows, dim = x.shape
    n_heads, _, head_dim = w_q.shape
    tile = min(rows, 256)
    row_block = lambda n: pl.BlockSpec((tile, n), lambda i: (i, 0))
    whole = lambda a: pl.BlockSpec(a.shape, lambda i: (0, 0, 0))
    return pl.pallas_call(
        qkv_kernel,
        out_shape=(jax.ShapeDtypeStruct((rows, n_heads * head_dim), jnp.bfloat16),
                   jax.ShapeDtypeStruct((rows, 2 * head_dim), jnp.bfloat16)),
        grid=(rows // tile,),
        in_specs=[row_block(dim), whole(w_q), whole(w_k), whole(w_v), row_block(head_dim), row_block(head_dim)],
        out_specs=(row_block(n_heads * head_dim), row_block(2 * head_dim)),
        compiler_params=pltpu.CompilerParams(dimension_semantics=("arbitrary",)),
        cost_estimate=pl.CostEstimate(flops=2 * rows * dim * (n_heads + 2) * head_dim, bytes_accessed=2 * (rows * dim + w_q.size), transcendentals=0),
    )(x, w_q, w_k, w_v, cos, sin)


def attn_kernel(cp, tp, chunk, groups, n_heads, scale2, cp_ref, q_ref, cos_ref, sin_ref, *refs):
    n_chunks = (len(refs) - 5)
    kv_refs = refs[:n_chunks]
    o_ref, qs, acc, m_ref, l_ref = refs[n_chunks:]
    half = tp // 2
    rows, hd = q_ref.shape[1], q_ref.shape[2] // n_heads
    t = pl.program_id(0)
    me = cp_ref[0]
    second = t >= half
    side = jnp.where(second, 1, 0)
    piece = jnp.where(second, 2 * cp - 1 - me, me)
    cosv, sinv = cos_ref[0], sin_ref[0]
    for h in range(n_heads):
        x = q_ref[0, :, h * hd:(h + 1) * hd].astype(jnp.float32)
        qs[h * rows:(h + 1) * rows, :] = (x * cosv + pltpu.roll(x, hd // 2, 1) * sinv).astype(jnp.bfloat16)
    acc[...] = jnp.zeros_like(acc)
    l_ref[...] = jnp.zeros_like(l_ref)
    m_ref[...] = jnp.full_like(m_ref, -1e30)
    total = rows * n_heads
    step = total // groups

    def update(tiles, mask):
        def score(g):
            q = qs[g * step:(g + 1) * step, :]
            out = [lax.dot_general(q, k, (((1,), (1,)), ((), ())), preferred_element_type=jnp.float32) for k, _ in tiles]
            if mask is not None:
                out[-1] = jnp.where(mask[g * step:(g + 1) * step], out[-1], -1e30)
            return out

        ahead = score(0)
        for g in range(groups):
            scores = ahead
            if g + 1 < groups:
                ahead = score(g + 1)
            sl = slice(g * step, (g + 1) * step)
            m_prev = m_ref[sl, :]
            m_cur = functools.reduce(jnp.maximum, [s[:, j * hd:(j + 1) * hd] for s in scores for j in range(s.shape[1] // hd)])
            m_new = jnp.maximum(m_prev, jnp.max(m_cur, axis=1, keepdims=True))
            alpha = jnp.exp2((m_prev - m_new) * scale2)
            l_new = l_ref[sl, :] * alpha
            a_new = acc[sl, :] * alpha
            for s, (_, v) in zip(scores, tiles):
                p = jnp.exp2((s - m_new[:, :1]) * scale2)
                for j in range(p.shape[1] // hd):
                    l_new = l_new + p[:, j * hd:(j + 1) * hd]
                a_new = a_new + jnp.dot(p.astype(jnp.bfloat16), v, preferred_element_type=jnp.float32)
            m_ref[sl, :] = m_new
            l_ref[sl, :] = l_new
            acc[sl, :] = a_new

    def load(i, j, lo, n):
        ref = kv_refs[i]
        if i < n_chunks - 1:
            j = lax.rem(me - j + cp, cp)
        k = ref[j, pl.ds(lo, n), :, :hd].reshape(n * rows, hd)
        v = ref[j, pl.ds(lo, n), :, hd:].reshape(n * rows, hd)
        return k, v

    def pair(parts):
        return (jnp.concatenate([p[0] for p in parts], axis=0), jnp.concatenate([p[1] for p in parts], axis=0))

    def full(p, carry):
        late = p >= cp
        j = jnp.where(late, 2 * cp - 1 - p, p)
        lo = jnp.where(late, half, 0)
        update([pair([load(i, j, lo, half) for i in range(n_chunks)])], None)
        return carry

    lax.fori_loop(0, piece, full, 0)
    lo = side * half

    def inner(tt, carry):
        update([pair([load(i, me, lo + tt, 1) for i in range(n_chunks)])], None)
        return carry

    lax.fori_loop(0, t - lo, inner, 0)
    n_keys = (chunk + 1) * rows
    qi = lax.broadcasted_iota(jnp.int32, (total, n_keys), 0) % rows + chunk * rows
    ki = lax.broadcasted_iota(jnp.int32, (total, n_keys), 1)
    update([pair([load(i, me, t, 1) for i in range(chunk + 1)])], qi >= ki)
    inv = 1.0 / jnp.sum(l_ref[...], axis=1, keepdims=True)
    for h in range(n_heads):
        sl = slice(h * rows, (h + 1) * rows)
        o_ref[0, :, h * hd:(h + 1) * hd] = (acc[sl, :] * inv[sl]).astype(o_ref.dtype)


def attention(q, cos, sin, kvs, me, cp, tp, chunk, n_heads, groups=5):
    _, rows, width = q.shape
    hd = width // n_heads
    scale2 = hd ** -0.5 * LOG2_E
    row_block = lambda n: pl.BlockSpec((1, rows, n), lambda t, s: (t, 0, 0))
    whole = pl.BlockSpec(kvs[0].shape, lambda t, s: (0, 0, 0, 0))
    return pl.pallas_call(
        functools.partial(attn_kernel, cp, tp, chunk, groups, n_heads, scale2),
        out_shape=jax.ShapeDtypeStruct(q.shape, jnp.bfloat16),
        grid_spec=pltpu.PrefetchScalarGridSpec(
            num_scalar_prefetch=1, grid=(tp,),
            in_specs=[row_block(width), row_block(hd), row_block(hd)] + [whole] * len(kvs),
            out_specs=row_block(width),
            scratch_shapes=[pltpu.VMEM((rows * n_heads, hd), jnp.bfloat16)] + [pltpu.VMEM((rows * n_heads, hd), jnp.float32)] * 3),
        compiler_params=pltpu.CompilerParams(dimension_semantics=("arbitrary",)),
        cost_estimate=pl.CostEstimate(flops=2 * 2 * rows * tp * n_heads * hd * rows * tp * 2, bytes_accessed=16 * 2 ** 20, transcendentals=0),
    )(me, q, cos, sin, *kvs)


def mlp_kernel(n_up, wide, x_ref, gate_ref, up_ref, down_ref, out_ref, hidden):
    i = pl.program_id(0)

    @pl.when(i < n_up)
    def _():
        weights = jnp.concatenate([gate_ref[...], up_ref[...]], axis=1)
        both = jnp.dot(x_ref[...], weights, preferred_element_type=jnp.float32)
        hidden[i] = (jax.nn.silu(both[:, :wide]) * both[:, wide:]).astype(jnp.bfloat16)

    @pl.when(i >= n_up)
    def _():
        h = jnp.concatenate([hidden[j] for j in range(n_up)], axis=1)
        out_ref[...] = jnp.dot(h, down_ref[...], preferred_element_type=jnp.float32).astype(jnp.bfloat16)


def mlp(x, w_gate, w_up, w_down, wide=384, cols=512):
    rows, dim = x.shape
    ffn = w_gate.shape[1]
    n_up, n_down = ffn // wide, dim // cols
    return pl.pallas_call(
        functools.partial(mlp_kernel, n_up, wide),
        out_shape=jax.ShapeDtypeStruct((rows, dim), jnp.bfloat16),
        grid=(n_up + n_down,),
        in_specs=[pl.BlockSpec((rows, dim), lambda i: (0, 0), pipeline_mode=pl.Buffered(1)),
                  pl.BlockSpec((dim, wide), lambda i: (0, jnp.minimum(i, n_up - 1))),
                  pl.BlockSpec((dim, wide), lambda i: (0, jnp.minimum(i, n_up - 1))),
                  pl.BlockSpec((ffn, cols), lambda i: (0, jnp.maximum(i - n_up, 0)))],
        out_specs=pl.BlockSpec((rows, cols), lambda i: (0, jnp.maximum(i - n_up, 0))),
        scratch_shapes=[pltpu.VMEM((n_up, rows, wide), jnp.bfloat16)],
        compiler_params=pltpu.CompilerParams(dimension_semantics=("arbitrary",)),
        cost_estimate=pl.CostEstimate(flops=6 * rows * dim * ffn, bytes_accessed=6 * dim * ffn, transcendentals=0),
    )(x, w_gate, w_up, w_down)


def up_kernel(wide, x_ref, gate_ref, up_ref, hidden_ref):
    weights = jnp.concatenate([gate_ref[...], up_ref[...]], axis=1)
    both = jnp.dot(x_ref[...], weights, preferred_element_type=jnp.float32)
    hidden_ref[...] = (jax.nn.silu(both[:, :wide]) * both[:, wide:]).astype(jnp.bfloat16)


def mlp_up(x, w_gate, w_up, wide=384):
    rows, dim = x.shape
    ffn = w_gate.shape[1]
    return pl.pallas_call(
        functools.partial(up_kernel, wide),
        out_shape=jax.ShapeDtypeStruct((rows, ffn), jnp.bfloat16),
        grid=(ffn // wide,),
        in_specs=[pl.BlockSpec((rows, dim), lambda i: (0, 0), pipeline_mode=pl.Buffered(1)),
                  pl.BlockSpec((dim, wide), lambda i: (0, i)), pl.BlockSpec((dim, wide), lambda i: (0, i))],
        out_specs=pl.BlockSpec((rows, wide), lambda i: (0, i)),
        compiler_params=pltpu.CompilerParams(dimension_semantics=("arbitrary",)),
        cost_estimate=pl.CostEstimate(flops=4 * rows * dim * ffn, bytes_accessed=4 * dim * ffn, transcendentals=0),
    )(x, w_gate, w_up)


def down_kernel(h_ref, down_ref, out_ref):
    out_ref[...] = jnp.dot(h_ref[...], down_ref[...], preferred_element_type=jnp.float32).astype(jnp.bfloat16)


def mlp_down(hidden, w_down, cols=512):
    rows, ffn = hidden.shape
    dim = w_down.shape[1]
    return pl.pallas_call(
        down_kernel,
        out_shape=jax.ShapeDtypeStruct((rows, dim), jnp.bfloat16),
        grid=(dim // cols,),
        in_specs=[pl.BlockSpec((rows, ffn), lambda i: (0, 0), pipeline_mode=pl.Buffered(1)),
                  pl.BlockSpec((ffn, cols), lambda i: (0, i))],
        out_specs=pl.BlockSpec((rows, cols), lambda i: (0, i)),
        compiler_params=pltpu.CompilerParams(dimension_semantics=("arbitrary",)),
        cost_estimate=pl.CostEstimate(flops=2 * rows * dim * ffn, bytes_accessed=2 * dim * ffn, transcendentals=0),
    )(hidden, w_down)


def solution(mesh):
    cp_size, tp_size = mesh.shape['cp'], mesh.shape['tp']
    row_spec = P('dp', ('cp', 'tp'), None)
    head_cols = P(None, 'tp', None)

    def local_layer(x, g_attn, w_q, w_k, w_v, w_o, g_mlp, w_gate, w_up, w_down):
        x_rows = x[0]
        n_own, dim = x_rows.shape
        n_heads, head_dim = w_q.shape[1], w_q.shape[2]
        cp_index = lax.axis_index('cp')
        seq_local = n_own * tp_size
        piece_len = seq_local // 2
        rows = n_own // N_CHUNKS
        wq_t, wk_t, wv_t = (jnp.transpose(w, (1, 0, 2)) for w in (w_q, w_k, w_v))
        w_o_flat = w_o.reshape(n_heads * head_dim, dim)

        within = jnp.arange(seq_local, dtype=jnp.int32)
        positions = jnp.where(within < piece_len, cp_index * piece_len + within,
                              (2 * cp_size - 1 - cp_index) * piece_len + within - piece_len)
        cos, sin = rope_tables(positions, head_dim)
        by_owner = lambda a: a.reshape(tp_size, N_CHUNKS, rows, a.shape[-1])
        cos, sin = by_owner(cos), by_owner(sin)

        normed = rms_norm(x_rows, g_attn)
        gathered = [lax.all_gather(normed[c * rows:(c + 1) * rows], 'tp', axis=0, tiled=True) for c in range(N_CHUNKS)]
        qs, kvs = [], []
        for c in range(N_CHUNKS):
            flat = lambda a: a[:, c].reshape(tp_size * rows, head_dim)
            q, kv = project_qkv(gathered[c], wq_t, wk_t, wv_t, flat(cos), flat(sin))
            qs.append(q.reshape(tp_size, rows, n_heads * head_dim))
            kv = kv.reshape(tp_size, rows, 2 * head_dim)
            if c == N_CHUNKS - 1:
                kvs.append(lax.all_gather(kv, 'cp', axis=0, tiled=False))
            else:
                shifted = [lax.ppermute(kv, 'cp', [(i, (i + d) % cp_size) for i in range(cp_size)]) for d in range(1, cp_size)]
                kvs.append(jnp.stack([kv] + shifted))
                gathered[c + 1], kvs[c] = lax.optimization_barrier((gathered[c + 1], kvs[c]))

        me = cp_index.astype(jnp.int32).reshape(1)
        sub = n_own // MLP_CHUNKS
        per = rows // sub
        mixed = [attention(qs[c], cos[:, c], sin[:, c], kvs, me, cp_size, tp_size, c, n_heads, 2) for c in range(N_CHUNKS)]

        def attn_out(mixed_c):
            return jnp.dot(mixed_c.reshape(tp_size * rows, n_heads * head_dim), w_o_flat,
                           preferred_element_type=jnp.float32).astype(jnp.bfloat16)

        def mlp_in(c, attn_rows):
            own = attn_rows[(c % per) * sub:(c % per + 1) * sub]
            resid = (x_rows[c * sub:(c + 1) * sub].astype(jnp.float32) + own.astype(jnp.float32)).astype(jnp.bfloat16)
            return resid, rms_norm(resid, g_mlp)

        scatter = lambda a: lax.psum_scatter(a, 'tp', scatter_dimension=0, tiled=True)
        gather = lambda a: lax.all_gather(a, 'tp', axis=0, tiled=True)
        whole_mlp = lambda a: mlp(a, w_gate, w_up, w_down)

        attn_0 = scatter(attn_out(mixed[0]))
        first = [mlp_in(c, attn_0) for c in range(per)]
        mixed_1, first = lax.optimization_barrier((mixed[1], first))
        arrived = [gather(r) for _, r in first]
        part_1, arrived[0] = lax.optimization_barrier((attn_out(mixed_1), arrived[0]))
        attn_1 = scatter(part_1)
        down_0, arrived[1] = lax.optimization_barrier((whole_mlp(arrived[0]), arrived[1]))
        down = [down_0]
        hidden = mlp_up(arrived[1], w_gate, w_up)
        hidden, attn_1 = lax.optimization_barrier((hidden, attn_1))
        later = [mlp_in(per + c, attn_1) for c in range(per)]
        hidden, later = lax.optimization_barrier((hidden, later))
        down.append(mlp_down(hidden, w_down))
        down += [whole_mlp(gather(r)) for _, r in later]
        resid = [r for r, _ in first + later]
        outs = [(r.astype(jnp.float32) + scatter(d).astype(jnp.float32)).astype(jnp.bfloat16) for r, d in zip(resid, down)]
        return jnp.concatenate(outs, axis=0)[None]

    return jax.shard_map(local_layer, mesh=mesh,
                         in_specs=(row_spec, P(), head_cols, head_cols, head_cols, P('tp', None, None),
                                   P(), P(None, 'tp'), P(None, 'tp'), P('tp', None)),
                         out_specs=row_spec, check_vma=False)
```

time: 1160 us -> 696 us (0.60)
  matrix products: 532 us -> 27.9 us
  Pallas kernels: 0 us -> 408 us
  waiting for transfers between devices: 425 us -> 201 us
  other arithmetic: 138 us -> 25.5 us
  local copies, waits for them, and re-layouts: 37.5 us -> 3.31 us
    dot_general x22 -> x2, matrix products: 513 us -> 27.9 us  [attn_out(): jnp.dot(mixed_c.reshape(tp_size * rows, n_heads * head_dim), w_o_flat, pr...]
    pallas_call x0 -> x9, Pallas kernels: none -> 408 us  [the longest x3 203 us: mlp(): pl.pallas_call(functools.partial(mlp_kernel, n_up, wide), out_shape=jax.S...]
    reduce_scatter x2 -> x6, waiting for transfers between devices: 217 us -> 56.9 us  [local_layer(): lax.psum_scatter(a, 'tp', scatter_dimension=0, tiled=True)]
    reduce_sum x8 -> x0, other arithmetic: 99.1 us -> none  [one_tile(): row_sum = jnp.sum(weights, axis=-1, keepdims=True)]
    all_gather x4 -> x7, waiting for transfers between devices: 207 us -> 119 us  [the longest x2 65.4 us: local_layer(): lax.all_gather(normed[c * rows:(c + 1) * rows], 'tp', axis=0, tiled=True)]
    ppermute x0 -> x3, waiting for transfers between devices: none -> 21.7 us  [local_layer(): lax.ppermute(kv, 'cp', [(i, (i + d) % cp_size) for i in range(cp_size)])]
    unnamed x1 -> x0, matrix products: 18.8 us -> none
    unnamed x16, local copies, waits for them, and re-layouts: 15 us -> 1.6 us
  transfers between devices with their start and end apart: 6 -> 16, of which waited for: 5 -> 10; matrix products, arithmetic and copies ran while one was open for 5% -> 4% of each run, Pallas kernels for 0% -> 50%
where the time goes in v1:
time: 696 us; the launch traced here: 686 us
  Pallas kernels  408 us (59%)
  waiting for transfers between devices  201 us (29%)
  matrix products  27.9 us (4%)
  other arithmetic  25.5 us (4%)
  between operations  13.9 us (2%)
    pallas_call x3, Pallas kernels, mlp(): pl.pallas_call(functools.partial(mlp_kernel, n_up, wide), out_shape=jax.S...  203 us
    pallas_call x2, Pallas kernels, attention(): pl.pallas_call(functools.partial(attn_kernel, cp, tp, chunk, groups, n_he...  102 us
    all_gather x2, waiting for transfers between devices, local_layer(): lax.all_gather(normed[c * rows:(c + 1) * rows], 'tp', axis=0, tiled=True)  65.4 us
    reduce_scatter x6, waiting for transfers between devices, local_layer(): lax.psum_scatter(a, 'tp', scatter_dimension=0, tiled=True)  56.9 us
    pallas_call x1, Pallas kernels, mlp_up(): pl.pallas_call(functools.partial(up_kernel, wide), out_shape=jax.ShapeDty...  43.9 us
    pallas_call x2, Pallas kernels, project_qkv(): pl.pallas_call(qkv_kernel, out_shape=(jax.ShapeDtypeStruct((rows, n_heads...  33.8 us
    dot_general x2, matrix products, attn_out(): jnp.dot(mixed_c.reshape(tp_size * rows, n_heads * head_dim), w_o_flat, pr...  27.9 us
    all_gather x1, waiting for transfers between devices, local_layer(): kvs.append(lax.all_gather(kv, 'cp', axis=0, tiled=False))  27.8 us
  transfers between devices with their start and end apart: 16, of which 10 were waited for; matrix products, arithmetic and copies ran while one was open for 4% of the time, Pallas kernels for 50%

profile of v1, /device:TPU:97, one launch (start us, length us, event | category | flops | bytes accessed | tf_op | source)
XLA Modules:
  0.0 686.0 jit_solution(3677776743720247931)
XLA Ops:
  6.6 0.7 convert_element_type.141
  7.3 2.5 fusion
  9.8 0.8 fusion.2
  10.6 1.7 fusion.27
  12.4 0.7 all-gather.8.cloned.1.call-update
  13.2 3.7 multiply_sine_fusion
  17.0 1.9 pad_maximum_fusion.1
  18.9 53.8 %all-gather.10.cloned.1.call-done.x_ref = bf16[1024,5120]{1,0:T(8,128)(2,1)} async-done(((bf16[128,5120]{1,0:T(8,128)(2,1)}), bf16[1024,5120]{1,0:T(8,128)(2,1)}) %all-gather.10.cloned.1.call-update) | async-done | bytes 10485776 | tf_op jit(solution)/shard_map/all_gather | solution.py:262
  72.7 16.9 %shard_map.100 = (bf16[1024,640]{1,0:T(8,128)(2,1)}, bf16[1024,256]{1,0:T(8,128)(2,1)}) custom-call(bf16[1024,5120]{1,0:T(8,128)(2,1)} %all-gather.10.cloned.1.call-done.x_ref, bf16[5,5120,128]{2,1,0:T(8,128)(2,1)} %bitcast.65, bf16[1,5120,128]{2,1,0:T(8,128)(2,1)} %bitcast.69, bf16[1,5120,128]{2,1,0:T(8,128)(2,1)} %bitcast.71, f32[1024,128]{1,0:T(8,128)} %bitcast.55, ...), custom_call_target="tpu_custom_call" | custom-call | flops 9395240960 | bytes 17039360 | tf_op jit(solution)/shard_map/pallas_call | solution.py:47
  89.6 1.2 collective-permute-start
  90.8 2.5 collective-permute-start.1
  93.2 1.3 collective-permute-start.2
  94.6 9.6 %collective-permute-done = bf16[8,128,256]{2,1,0:T(8,128)(2,1)S(1)} collective-permute-done((bf16[8,128,256]{2,1,0:T(8,128)(2,1)}, bf16[8,128,256]{2,1,0:T(8,128)(2,1)S(1)}, u32[]{:S(2)}, u32[]{:S(2)}) %collective-permute-start) | collective-permute-done | bytes 524320 | tf_op jit(solution)/shard_map/ppermute | solution.py:272
  104.1 12.1 %collective-permute-done.1 = bf16[8,128,256]{2,1,0:T(8,128)(2,1)S(1)} collective-permute-done((bf16[8,128,256]{2,1,0:T(8,128)(2,1)}, bf16[8,128,256]{2,1,0:T(8,128)(2,1)S(1)}, u32[]{:S(2)}, u32[]{:S(2)}) %collective-permute-start.1) | collective-permute-done | bytes 524320 | tf_op jit(solution)/shard_map/ppermute | solution.py:272
  116.2 2.6 pad_maximum_fusion.refs_0_
  118.9 11.6 %all-gather.8.cloned.1.call-done.x_ref = bf16[1024,5120]{1,0:T(8,128)(2,1)} async-done(((bf16[128,5120]{1,0:T(8,128)(2,1)}), bf16[1024,5120]{1,0:T(8,128)(2,1)}) %all-gather.8.cloned.1.call-update) | async-done | bytes 10485776 | tf_op jit(solution)/shard_map/all_gather | solution.py:262
  130.5 16.9 %shard_map.101 = (bf16[1024,640]{1,0:T(8,128)(2,1)}, bf16[1024,256]{1,0:T(8,128)(2,1)}) custom-call(bf16[1024,5120]{1,0:T(8,128)(2,1)} %all-gather.8.cloned.1.call-done.x_ref, bf16[5,5120,128]{2,1,0:T(8,128)(2,1)} %bitcast.66, bf16[1,5120,128]{2,1,0:T(8,128)(2,1)} %bitcast.70, bf16[1,5120,128]{2,1,0:T(8,128)(2,1)} %bitcast.72, f32[1024,128]{1,0:T(8,128)} %bitcast.51, ...), custom_call_target="tpu_custom_call" | custom-call | flops 9395240960 | bytes 17039360 | tf_op jit(solution)/shard_map/pallas_call | solution.py:47
  147.5 27.8 %all-gather.12.cloned.1.call-done.refs_1_ = bf16[4,8,128,256]{3,2,1,0:T(8,128)(2,1)} async-done(((bf16[1,8,128,256]{3,2,1,0:T(8,128)(2,1)}), bf16[4,8,128,256]{3,2,1,0:T(8,128)(2,1)}) %all-gather.12.cloned.1.call-update) | async-done | bytes 2097168 | tf_op jit(solution)/shard_map/all_gather | solution.py:270
  175.3 50.5 %shard_map.103 = bf16[8,128,640]{2,1,0:T(8,128)(2,1)} custom-call(s32[1]{0:T(128)} %bitcast.cp_ref, bf16[8,128,640]{2,1,0:T(8,128)(2,1)} %bitcast.73, f32[8,128,128]{2,1,0:T(8,128)} %bitcast.56, f32[8,128,128]{2,1,0:T(8,128)} %bitcast.54, bf16[4,8,128,256]{3,2,1,0:T(8,128)(2,1)} %pad_maximum_fusion.refs_0_, ...), custom_call_target="tpu_custom_call" | custom-call | flops 5368709120 | bytes 16777216 | tf_op jit(solution)/shard_map/pallas_call | solution.py:151
  225.8 14.0 %convolution_convert_fusion.1 = bf16[1024,5120]{1,0:T(8,128)(2,1)} fusion(bf16[1024,640]{1,0:T(8,128)(2,1)} %bitcast.76, bf16[640,5120]{1,0:T(8,128)(2,1)} %bitcast.67), kind=kOutput, calls=%fused_computation.1 | convolution fusion | flops 6716129280 | bytes 18350080 | tf_op jit(solution)/shard_map/dot_general | solution.py:282
  239.9 0.6 copy-done.7
  240.5 51.7 %shard_map.102 = bf16[8,128,640]{2,1,0:T(8,128)(2,1)} custom-call(s32[1]{0:T(128)} %bitcast.cp_ref, bf16[8,128,640]{2,1,0:T(8,128)(2,1)} %bitcast.75, f32[8,128,128]{2,1,0:T(8,128)} %bitcast.52, f32[8,128,128]{2,1,0:T(8,128)} %bitcast.50, bf16[4,8,128,256]{3,2,1,0:T(8,128)(2,1)} %pad_maximum_fusion.refs_0_, ...), custom_call_target="tpu_custom_call" | custom-call | flops 5368709120 | bytes 16777216 | tf_op jit(solution)/shard_map/pallas_call | solution.py:151
  292.2 7.6 %reduce-scatter.7.cloned.1.call-done = bf16[128,5120]{1,0:T(8,128)(2,1)} async-done(((bf16[1024,5120]{1,0:T(8,128)(2,1)}), bf16[128,5120]{1,0:T(8,128)(2,1)}) %reduce-scatter.7.cloned.1.call-update) | async-done | bytes 1310736 | tf_op jit(solution)/shard_map/reduce_scatter | solution.py:290
  299.7 1.8 fusion.6
  301.6 1.5 fusion.8
  303.2 0.6 all-gather.16.cloned.1.call-update
  303.8 0.3 reduce-scatter.11.cloned.1.call-start
  304.1 14.0 %convolution_convert_fusion = bf16[1024,5120]{1,0:T(8,128)(2,1)} fusion(bf16[1024,640]{1,0:T(8,128)(2,1)} %bitcast.74, bf16[640,5120]{1,0:T(8,128)(2,1)} %bitcast.68), kind=kOutput, calls=%fused_computation | convolution fusion | flops 6716129280 | bytes 18350080 | tf_op jit(solution)/shard_map/dot_general | solution.py:282
  318.1 19.3 %all-gather.14.cloned.1.call-done.x_ref = bf16[512,5120]{1,0:T(8,128)(2,1)} async-done(((bf16[64,5120]{1,0:T(8,128)(2,1)}), bf16[512,5120]{1,0:T(8,128)(2,1)}) %all-gather.14.cloned.1.call-update) | async-done | bytes 5242896 | tf_op jit(solution)/shard_map/all_gather | solution.py:291
  337.5 67.7 %shard_map.104 = bf16[512,5120]{1,0:T(8,128)(2,1)} custom-call(bf16[512,5120]{1,0:T(8,128)(2,1)} %all-gather.14.cloned.1.call-done.x_ref, bf16[5120,3456]{1,0:T(8,128)(2,1)} %gate_ref.7, bf16[5120,3456]{1,0:T(8,128)(2,1)} %up_ref.7, bf16[3456,5120]{1,0:T(8,128)(2,1)} %down_ref.7), custom_call_target="tpu_custom_call" | custom-call | flops 54358179840 | bytes 106168320 | tf_op jit(solution)/shard_map/pallas_call | solution.py:183
  405.3 43.9 %shard_map.105.h_ref = bf16[512,3456]{1,0:T(8,128)(2,1)} custom-call(bf16[512,5120]{1,0:T(8,128)(2,1)} %all-gather.16.cloned.1.call-done.x_ref, bf16[5120,3456]{1,0:T(8,128)(2,1)} %gate_ref.7, bf16[5120,3456]{1,0:T(8,128)(2,1)} %up_ref.7), custom_call_target="tpu_custom_call" | custom-call | flops 36238786560 | bytes 70778880 | tf_op jit(solution)/shard_map/pallas_call | solution.py:207
  449.1 1.8 fusion.12
  451.0 1.5 fusion.14
  452.6 0.7 all-gather.20.cloned.1.call-update
  453.4 0.6 reduce-scatter.9.cloned.1.call-update
  454.1 25.2 %shard_map.106 = bf16[512,5120]{1,0:T(8,128)(2,1)} custom-call(bf16[512,3456]{1,0:T(8,128)(2,1)} %shard_map.105.h_ref, bf16[3456,5120]{1,0:T(8,128)(2,1)} %down_ref.7), custom_call_target="tpu_custom_call" | custom-call | flops 18119393280 | bytes 35389440 | tf_op jit(solution)/shard_map/pallas_call | solution.py:226
  479.3 0.3 reduce-scatter.15.cloned.1.call-start
  479.7 6.8 all-gather.18.cloned.1.call-done.x_ref
  486.4 67.5 %shard_map.107 = bf16[512,5120]{1,0:T(8,128)(2,1)} custom-call(bf16[512,5120]{1,0:T(8,128)(2,1)} %all-gather.18.cloned.1.call-done.x_ref, bf16[5120,3456]{1,0:T(8,128)(2,1)} %gate_ref.7, bf16[5120,3456]{1,0:T(8,128)(2,1)} %up_ref.7, bf16[3456,5120]{1,0:T(8,128)(2,1)} %down_ref.7), custom_call_target="tpu_custom_call" | custom-call | flops 54358179840 | bytes 106168320 | tf_op jit(solution)/shard_map/pallas_call | solution.py:183
  554.1 67.8 %shard_map.108 = bf16[512,5120]{1,0:T(8,128)(2,1)} custom-call(bf16[512,5120]{1,0:T(8,128)(2,1)} %all-gather.20.cloned.1.call-done.x_ref, bf16[5120,3456]{1,0:T(8,128)(2,1)} %gate_ref.7, bf16[5120,3456]{1,0:T(8,128)(2,1)} %up_ref.7, bf16[3456,5120]{1,0:T(8,128)(2,1)} %down_ref.7), custom_call_target="tpu_custom_call" | custom-call | flops 54358179840 | bytes 106168320 | tf_op jit(solution)/shard_map/pallas_call | solution.py:183
  622.0 1.0 copy-done.4
  623.0 1.2 add_convert_fusion.3
  624.3 1.3 add_convert_fusion.2
  625.6 11.4 %reduce-scatter.15.cloned.1.call-done = bf16[64,5120]{1,0:T(8,128)(2,1)} async-done(((bf16[512,5120]{1,0:T(8,128)(2,1)}), bf16[64,5120]{1,0:T(8,128)(2,1)}) %reduce-scatter.15.cloned.1.call-update) | async-done | bytes 655376 | tf_op jit(solution)/shard_map/reduce_scatter | solution.py:290
  636.9 1.2 add_convert_fusion.1
  638.2 38.0 %reduce-scatter.17.cloned.1.call-done = bf16[64,5120]{1,0:T(8,128)(2,1)} async-done(((bf16[512,5120]{1,0:T(8,128)(2,1)}), bf16[64,5120]{1,0:T(8,128)(2,1)}) %reduce-scatter.17.cloned.1.call-update) | async-done | bytes 655376 | tf_op jit(solution)/shard_map/reduce_scatter | solution.py:290
  676.1 1.2 add_convert_fusion
  677.4 1.6 maximum_bitcast_fusion
  (48 shorter events, 1.3 us)
Async XLA Ops:
  6.5 66.1 %all-gather.10.cloned.1.call-start = ((), (), s32[]{:S(2)}) async-start(), calls=%async_computation.7 | async-start | bytes 11796480 | tf_op jit(solution)/shard_map/all_gather | solution.py:262
  7.3 2.5 copy-start
  12.3 118.1 %all-gather.8.cloned.1.call-start = ((), (), s32[]{:S(2)}) async-start(), calls=%async_computation.6 | async-start | bytes 11796480 | tf_op jit(solution)/shard_map/all_gather | solution.py:262
  13.1 162.2 %all-gather.12.cloned.1.call-start = ((), (), s32[]{:S(2)}) async-start(), calls=%async_computation.8 | async-start | bytes 2621440 | tf_op jit(solution)/shard_map/all_gather | solution.py:270
  89.6 14.5 %collective-permute-start = (bf16[8,128,256]{2,1,0:T(8,128)(2,1)}, bf16[8,128,256]{2,1,0:T(8,128)(2,1)S(1)}, u32[]{:S(2)}, u32[]{:S(2)}) collective-permute-start(bf16[8,128,256]{2,1,0:T(8,128)(2,1)} %bitcast.58), channel_id=1, source_target_pairs={{0,8},{8,16},{16,24},{24,0},{1,9},{9,17},{17,25},{25,1},{2,10},{10... | collective-permute-start | bytes 1572872 | tf_op jit(solution)/shard_map/ppermute | solution.py:272
  90.8 25.4 %collective-permute-start.1 = (bf16[8,128,256]{2,1,0:T(8,128)(2,1)}, bf16[8,128,256]{2,1,0:T(8,128)(2,1)S(1)}, u32[]{:S(2)}, u32[]{:S(2)}) collective-permute-start(bf16[8,128,256]{2,1,0:T(8,128)(2,1)} %bitcast.59), channel_id=1, source_target_pairs={{0,16},{8,24},{16,0},{24,8},{1,17},{9,25},{17,1},{25,9},{2,18},{10... | collective-permute-start | bytes 1572872 | tf_op jit(solution)/shard_map/ppermute | solution.py:272
  93.2 23.0 %collective-permute-start.2 = (bf16[8,128,256]{2,1,0:T(8,128)(2,1)}, bf16[8,128,256]{2,1,0:T(8,128)(2,1)S(1)}, u32[]{:S(2)}, u32[]{:S(2)}) collective-permute-start(bf16[8,128,256]{2,1,0:T(8,128)(2,1)} %bitcast.60), channel_id=1, source_target_pairs={{0,24},{8,0},{16,8},{24,16},{1,25},{9,1},{17,9},{25,17},{2,26},{10... | collective-permute-start | bytes 1572872 | tf_op jit(solution)/shard_map/ppermute | solution.py:272
  147.4 152.3 %reduce-scatter.7.cloned.1.call-start = ((), (), s32[]{:S(2)}) async-start(), calls=%async_computation.9 | async-start | bytes 11796480 | tf_op jit(solution)/shard_map/reduce_scatter | solution.py:290
  239.8 0.7 copy-start.7
  239.9 97.5 %all-gather.14.cloned.1.call-start = ((), (), s32[]{:S(2)}) async-start(), calls=%async_computation.10 | async-start | bytes 5898240 | tf_op jit(solution)/shard_map/all_gather | solution.py:291
  301.6 1.5 copy-start.1
  301.6 1.5 copy-start.3
  303.2 102.1 %all-gather.16.cloned.1.call-start = ((), (), s32[]{:S(2)}) async-start(), calls=%async_computation.11 | async-start | bytes 5898240 | tf_op jit(solution)/shard_map/all_gather | solution.py:291
  303.8 145.3 %reduce-scatter.11.cloned.1.call-start = ((), (), s32[]{:S(2)}) async-start(), calls=%async_computation.13 | async-start | bytes 11796480 | tf_op jit(solution)/shard_map/reduce_scatter | solution.py:290
  337.5 149.0 %all-gather.18.cloned.1.call-start = ((), (), s32[]{:S(2)}) async-start(), calls=%async_computation.15 | async-start | bytes 5898240 | tf_op jit(solution)/shard_map/all_gather | solution.py:291
  451.0 1.5 copy-start.5
  452.5 101.6 %all-gather.20.cloned.1.call-start = ((), (), s32[]{:S(2)}) async-start(), calls=%async_computation.17 | async-start | bytes 5898240 | tf_op jit(solution)/shard_map/all_gather | solution.py:291
  453.3 168.7 %reduce-scatter.9.cloned.1.call-start = ((), (), s32[]{:S(2)}) async-start(), calls=%async_computation.12 | async-start | bytes 5898240 | tf_op jit(solution)/shard_map/reduce_scatter | solution.py:290
  454.0 170.3 %reduce-scatter.13.cloned.1.call-start = ((), (), s32[]{:S(2)}) async-start(), calls=%async_computation.14 | async-start | bytes 5898240 | tf_op jit(solution)/shard_map/reduce_scatter | solution.py:290
  479.3 157.6 %reduce-scatter.15.cloned.1.call-start = ((), (), s32[]{:S(2)}) async-start(), calls=%async_computation.16 | async-start | bytes 5898240 | tf_op jit(solution)/shard_map/reduce_scatter | solution.py:290
  554.0 122.1 %reduce-scatter.17.cloned.1.call-start = ((), (), s32[]{:S(2)}) async-start(), calls=%async_computation.18 | async-start | bytes 5898240 | tf_op jit(solution)/shard_map/reduce_scatter | solution.py:290
  621.9 1.1 copy-start.4
  622.0 2.3 copy-start.2
  624.2 12.7 %copy-start.6 = (bf16[64,5120]{1,0:T(8,128)(2,1)S(1)}, bf16[64,5120]{1,0:T(8,128)(2,1)}, u32[]{:S(2)}) copy-start(bf16[64,5120]{1,0:T(8,128)(2,1)} %copy-done.5) | copy-start | bytes 1966084
Sparse Core Ops, SparseCore 0:
  12.4 60.1 all-gather.9
  74.2 56.1 all-gather.7
  147.6 27.7 all-gather.11
  240.0 59.6 reduce-scatter.6
  303.3 34.0 all-gather.13
  338.9 33.6 all-gather.15
  374.9 59.1 reduce-scatter.10
  452.7 33.7 all-gather.17
  488.0 33.6 all-gather.19
  523.9 34.6 reduce-scatter.8
  560.9 36.8 reduce-scatter.12
  600.0 36.8 reduce-scatter.14
  639.2 36.8 reduce-scatter.16
